TPU v7x, 16 devices: a 4x2x1 block of a 4x4x8 slice. The times are simulated.
16 devices in a mesh: rep: 2 (over y, z), dp: 8 (over x, core).
Axes of the slice: x: 4, y: 2, z: 1, core: 2. Of those that a mesh axis runs over, the one named last changes fastest.
The devices are a block of a 4x4x8 slice.
Arguments:
- a: bfloat16 [16, 4, 4096, 512], P(('rep', 'dp')), parts along dimension 0
- g: bfloat16 [16, 4, 4096, 2048], P(('rep', 'dp')), parts along dimension 0
Outputs:
- output: bfloat16 [8, 512, 2048], P('rep'), parts along dimension 0
There are 2 independent parts. A program takes and returns all parts, laid end to end along the dimension named above; each array names one.
All inputs are finite; a program needn't handle non-finite values.
Results may differ from a plain program's by a relative error of at most 0.012.
Values are sent between devices in bfloat16 or wider.
A program may use at most 768 MiB of HBM per device.

v0:
```python
import jax
import jax.numpy as jnp


def solution(mesh):
    groups = mesh.shape["rep"]

    def step(a, g):
        a, g = (t.reshape(groups, -1, *t.shape[1:]) for t in (a, g))
        sums = jnp.einsum("rsntd,rsntf->rndf", a, g, preferred_element_type=jnp.float32)
        return sums.astype(jnp.bfloat16).reshape(-1, *sums.shape[2:])

    return step
```

profile of v0, /device:TPU:113, one launch (start us, length us, event | category | flops | bytes accessed | tf_op | source)
XLA Modules:
  0.0 219.1 jit_solution(2484521718213935370)
XLA Ops:
  0.0 45.1 %fusion.3 = f32[1,4,512,2048]{3,2,1,0:T(8,128)} fusion(bf16[1,4,4096,2048]{3,2,1,0:T(8,128)(2,1)} %param.1, bf16[1,4,4096,512]{3,2,1,0:T(8,128)(2,1)} %param), kind=kOutput, calls=%fused_computation.4 | convolution fusion | flops 34359738368 | bytes 100663296 | tf_op jit(solution)/rsntd,rsntf->rndf/dot_general | solution.py:10
  45.1 174.0 %all-reduce.2 = bf16[1,4,512,2048]{3,2,1,0:T(8,128)(2,1)} all-reduce(f32[1,4,512,2048]{3,2,1,0:T(8,128)} %fusion.3), channel_id=1, replica_groups=[2,8]<=[16], use_global_device_ids=true, to_apply=%add.clone | all-reduce | flops 4194304 | bytes 25165824 | tf_op jit(solution)/rsntd,rsntf->rndf/dot_general | solution.py:10
where the time goes:
time: 221 us; the launch traced here: 219 us
  blocking collectives  174 us (79%)
  matrix products  45.1 us (20%)
    dot_general x1, blocking collectives, step(): jnp.einsum('rsntd,rsntf->rndf', a, g, preferred_element_type=jnp.float32)  174 us
    dot_general x1, matrix products, step(): jnp.einsum('rsntd,rsntf->rndf', a, g, preferred_element_type=jnp.float32)  45.1 us

commit v1 on v0

v1 whole, which is shorter than its diff:
```python
import functools

import jax
import jax.numpy as jnp
from jax import lax
from jax.experimental import pallas as pl
from jax.experimental.pallas import tpu as pltpu
from jax.sharding import PartitionSpec as P

MESH = pl.DeviceIdType.MESH
BLOCK = 512
ACCS = 8
LAG2, LAG3, LAG4, LAG5 = 1, 2, 5, 8


def kernel(
    chips,
    a_hbm,
    g_hbm,
    out,
    abuf,
    gbuf,
    acc,
    give,
    take,
    stage,
    part,
    whole,
    a_sem,
    g_sem,
    give_sem,
    take_sem,
    stage_sem,
    part_sem,
    whole_sem,
    own_sem,
    near_sem,
    pass_sem,
    far_sem,
    last_sem,
    done_sem,
):
    matrices, rows, columns = out.shape
    blocks = columns // BLOCK
    pieces = matrices * blocks
    half = rows // 2
    chunk = half // chips
    h = chunk // 2

    me = lax.axis_index("dp")
    chip, core = me // 2, me % 2
    other = chip * 2 + 1 - core
    nxt, prv = (chip + 1) % chips, (chip + chips - 1) % chips
    opp = (chip + 2) % chips
    right, left = nxt * 2 + core, prv * 2 + core
    to = (right, left)

    def a_copy(n):
        return pltpu.make_async_copy(a_hbm.at[0, n], abuf.at[n % 2], a_sem.at[n % 2])

    def g_copy(p):
        cols = pl.ds(pl.multiple_of(p % blocks * BLOCK, BLOCK), BLOCK)
        return pltpu.make_async_copy(g_hbm.at[0, p // blocks, :, cols], gbuf.at[p % 3], g_sem.at[p % 3])

    def send(src, dst, send_sem, recv_sem, device):
        return pltpu.make_async_remote_copy(
            src_ref=src,
            dst_ref=dst,
            send_sem=send_sem,
            recv_sem=recv_sem,
            device_id={"dp": device},
            device_id_type=MESH,
        )

    def rows_of(first, size):
        return pl.ds(pl.multiple_of(first, h), size)

    def in_out(p, first, size):
        cols = pl.ds(pl.multiple_of(p % blocks * BLOCK, BLOCK), BLOCK)
        return out.at[p // blocks, pl.ds(pl.multiple_of(core * half + first, h), size), cols]

    def exchange(p):
        return send(give.at[p], take.at[p], give_sem, take_sem.at[p], other)

    def part_copy(p, way):
        src = stage.at[p, pl.ds(2 * chunk + way * h, h)]
        return send(src, part.at[p, way], stage_sem, part_sem.at[p, way], to[way])

    def whole_copy(p, way, piece_half):
        src = stage.at[p, pl.ds(way * chunk + piece_half * h, h)]
        dst = whole.at[p, way, pl.ds(piece_half * h, h)]
        return send(src, dst, stage_sem, whole_sem.at[p, way], to[way])

    def own_copy(p, way):
        where = in_out(p, chip * chunk, chunk)
        return send(where, where, own_sem, near_sem.at[p, way], to[way])

    def pass_copy(p, way):
        where = in_out(p, (prv, nxt)[way] * chunk + way * h, h)
        return send(where, where, pass_sem, far_sem.at[p, way], to[way])

    def last_copy(p):
        where = in_out(p, 0, half)
        return send(where, where, last_sem, done_sem, other)

    def wait_all(ref, sem):
        pltpu.make_async_copy(ref, ref, sem).wait()

    a_copy(0).start()
    g_copy(0).start()
    g_copy(1).start()

    barrier = pltpu.get_barrier_semaphore()
    for device in (other, right, left):
        pl.semaphore_signal(barrier, inc=1, device_id={"dp": device}, device_id_type=MESH)
    pl.semaphore_wait(barrier, 3)

    @pl.loop(0, pieces + LAG5)
    def _(s):
        @pl.when(s < pieces)
        def _():
            p, n, c = s, s // blocks, s % blocks

            @pl.when(p + 2 < pieces)
            def _():
                g_copy(p + 2).start()

            @pl.when((c == 0) & (n + 1 < matrices))
            def _():
                a_copy(n + 1).start()

            @pl.when(c == 0)
            def _():
                a_copy(n).wait()

            g_copy(p).wait()

            def product(owner):
                mine = pl.ds(pl.multiple_of(owner * half, half), half)
                return lax.dot_general(
                    abuf[n % 2, :, mine],
                    gbuf[p % 3],
                    (((0,), (0,)), ((), ())),
                    preferred_element_type=jnp.float32,
                )

            give[p] = product(1 - core).astype(give.dtype)
            exchange(p).start()
            acc[p % ACCS] = product(core)

        @pl.when((s >= LAG2) & (s < pieces + LAG2))
        def _():
            p = s - LAG2
            for way in range(2):
                part_copy(p, way).wait_recv()
                mine = acc[p % ACCS, rows_of((nxt, prv)[way] * chunk + way * h, h)]
                total = mine + part[p, way].astype(jnp.float32)
                stage[p, pl.ds(way * chunk + way * h, h)] = total.astype(stage.dtype)
                whole_copy(p, way, way).start()

        @pl.when(s < pieces)
        def _():
            p = s
            exchange(p).wait_recv()

            def total(first, size):
                where = rows_of(first, size)
                return acc[p % ACCS, where] + take[p, where].astype(jnp.float32)

            stage[p, pl.ds(2 * chunk, chunk)] = total(opp * chunk, chunk).astype(stage.dtype)
            for way in range(2):
                part_copy(p, way).start()
            for way in range(2):
                rest = (nxt, prv)[way] * chunk + (1 - way) * h
                stage[p, pl.ds(way * chunk + (1 - way) * h, h)] = total(rest, h).astype(stage.dtype)
                whole_copy(p, way, 1 - way).start()
            for way in range(2):
                first = (nxt, prv)[way] * chunk + way * h
                acc[p % ACCS, rows_of(first, h)] = total(first, h)
            acc[p % ACCS, rows_of(chip * chunk, chunk)] = total(chip * chunk, chunk)

        @pl.when((s >= LAG3) & (s < pieces + LAG3))
        def _():
            p = s - LAG3
            for way in range(2):
                wait = whole.at[p, way]
                send(wait, wait, stage_sem, whole_sem.at[p, way], to[way]).wait_recv()
            total = acc[p % ACCS, rows_of(chip * chunk, chunk)]
            total = total + whole[p, 0].astype(jnp.float32) + whole[p, 1].astype(jnp.float32)
            in_out(p, chip * chunk, chunk)[...] = total.astype(out.dtype)
            for way in range(2):
                own_copy(p, way).start()

        @pl.when((s >= LAG4) & (s < pieces + LAG4))
        def _():
            p = s - LAG4
            for way in range(2):
                own_copy(p, way).wait_recv()
                pass_copy(p, way).start()

        @pl.when(s >= LAG5)
        def _():
            p = s - LAG5
            for way in range(2):
                pass_copy(p, way).wait_recv()
            last_copy(p).start()

    wait_all(give, give_sem)
    wait_all(stage, stage_sem)
    wait_all(whole, own_sem)
    wait_all(part, pass_sem)
    wait_all(take, last_sem)
    wait_all(take, done_sem)


def solution(mesh):
    chips = mesh.shape["dp"] // 2

    def step(a, g):
        _, matrices, tokens, rows = a.shape
        columns = g.shape[-1]
        pieces = matrices * (columns // BLOCK)
        half = rows // 2
        chunk = half // chips
        vmem = lambda *shape: pltpu.VMEM(shape, jnp.bfloat16)
        dma = pltpu.SemaphoreType.DMA
        return pl.pallas_call(
            functools.partial(kernel, chips),
            out_shape=jax.ShapeDtypeStruct((matrices, rows, columns), jnp.bfloat16),
            in_specs=[pl.BlockSpec(memory_space=pl.ANY)] * 2,
            out_specs=pl.BlockSpec(memory_space=pltpu.VMEM),
            scratch_shapes=[
                vmem(2, tokens, rows),
                vmem(3, tokens, BLOCK),
                pltpu.VMEM((ACCS, half, BLOCK), jnp.float32),
                vmem(pieces, half, BLOCK),
                vmem(pieces, half, BLOCK),
                vmem(pieces, 3 * chunk, BLOCK),
                vmem(pieces, 2, chunk // 2, BLOCK),
                vmem(pieces, 2, chunk, BLOCK),
                dma((2,)),
                dma((3,)),
                dma,
                dma((pieces,)),
                dma,
                dma((pieces, 2)),
                dma((pieces, 2)),
                dma,
                dma((pieces, 2)),
                dma,
                dma((pieces, 2)),
                dma,
                dma,
            ],
            compiler_params=pltpu.CompilerParams(
                collective_id=0, has_side_effects=True, vmem_limit_bytes=63 * 2**20
            ),
            name="grad_sums",
        )(a, g)

    return jax.shard_map(
        step,
        mesh=mesh,
        in_specs=(P(("rep", "dp")), P(("rep", "dp"))),
        out_specs=P("rep"),
        check_vma=False,
    )
```

time: 221 us -> 98.8 us (0.45)
  blocking collectives: 174 us -> 0 us
  Pallas kernels: 0 us -> 90.2 us
  matrix products: 45.1 us -> 0 us
  local copies, waits for them, and re-layouts: 0 us -> 8.44 us
    dot_general x1 -> x0, blocking collectives: 174 us -> none  [step(): jnp.einsum('rsntd,rsntf->rndf', a, g, preferred_element_type=jnp.float32)]
    pallas_call x0 -> x1, Pallas kernels: none -> 90.2 us  [step(): pl.pallas_call(functools.partial(kernel, chips), out_shape=jax.ShapeDtype...]
    dot_general x1 -> x0, matrix products: 45.1 us -> none  [step(): jnp.einsum('rsntd,rsntf->rndf', a, g, preferred_element_type=jnp.float32)]
    unnamed x0 -> x1, local copies, waits for them, and re-layouts: none -> 8.44 us
where the time goes in v1:
time: 98.8 us; the launch traced here: 98.7 us
  Pallas kernels  90.2 us (91%)
  local copies, waits for them, and re-layouts  8.44 us (9%)
    pallas_call x1, Pallas kernels, step(): pl.pallas_call(functools.partial(kernel, chips), out_shape=jax.ShapeDtype...  90.2 us
    unnamed x1, local copies, waits for them, and re-layouts  8.44 us

profile of v1, /device:TPU:113, one launch (start us, length us, event | category | flops | bytes accessed | tf_op | source)
XLA Modules:
  0.0 98.7 jit_solution(15273637064774214508)
XLA Ops:
  0.0 90.2 %grad_sums.1 = bf16[4,512,2048]{2,1,0:T(8,128)(2,1)} custom-call(bf16[1,4,4096,512]{3,2,1,0:T(8,128)(2,1)} %a_hbm.1, bf16[1,4,4096,2048]{3,2,1,0:T(8,128)(2,1)} %g_hbm.1), custom_call_target="tpu_custom_call" | custom-call | tf_op jit(solution)/shard_map/grad_sums/pallas_call | solution.py:227
  90.2 8.4 %copy.4 = bf16[4,512,2048]{2,1,0:T(8,128)(2,1)} copy(bf16[4,512,2048]{2,1,0:T(8,128)(2,1)} %grad_sums.1) | data formatting | bytes 16777216

commit v2 on v1

v2 whole, which is shorter than its diff:
```python
import functools

import jax
import jax.numpy as jnp
from jax import lax
from jax.experimental import pallas as pl
from jax.experimental.pallas import tpu as pltpu
from jax.sharding import PartitionSpec as P

MESH = pl.DeviceIdType.MESH
BLOCK = 512
ACCS = 4
HEAD = 4
PARTS, WHOLES = 6, 12
SPARSE = 4
DENSE = 15, 3
GATHER = 17
CLOSE = 20

def kernel(
    chips,
    a_hbm,
    g_hbm,
    out,
    abuf,
    gbuf,
    acc,
    kept,
    give,
    take,
    stage,
    part,
    whole,
    head_sem,
    a_sem,
    g_sem,
    give_sem,
    take_sem,
    stage_sem,
    part_sem,
    whole_sem,
    own_sem,
    near_sem,
    pass_sem,
    far_sem,
    last_sem,
    done_sem,
):
    matrices, rows, columns = out.shape
    tokens = abuf.shape[1]
    blocks = columns // BLOCK
    pieces = matrices * blocks
    half = rows // 2
    chunk = half // chips
    h = chunk // 2

    me = lax.axis_index("dp")
    chip, core = me // 2, me % 2
    other = chip * 2 + 1 - core
    nxt, prv = (chip + 1) % chips, (chip + chips - 1) % chips
    opp = (chip + 2) % chips
    right, left = nxt * 2 + core, prv * 2 + core
    to = (right, left)
    beside = (nxt, prv)

    class Piece:
        def __init__(self, p):
            self.p = p
            self.n = p // blocks
            self.acc = p % ACCS
            self.cols = pl.ds(pl.multiple_of(p % blocks * BLOCK, BLOCK), BLOCK)

        def in_out(self, row, size):
            return out.at[self.n, pl.ds(pl.multiple_of(core * half + row, h), size), self.cols]

    def a_copy(n):
        return pltpu.make_async_copy(a_hbm.at[0, n], abuf.at[n % 2], a_sem.at[n % 2])

    def g_copy(p):
        cols = pl.ds(pl.multiple_of(p % blocks * BLOCK, BLOCK), BLOCK)
        return pltpu.make_async_copy(g_hbm.at[0, p // blocks, :, cols], gbuf.at[p % 3], g_sem.at[p % 3])

    def head_copies(k):
        size = tokens // HEAD
        some = pl.ds(k * size, size)
        return (
            pltpu.make_async_copy(a_hbm.at[0, 0, some], abuf.at[0, some], head_sem.at[k]),
            pltpu.make_async_copy(g_hbm.at[0, 0, some, pl.ds(0, BLOCK)], gbuf.at[0, some], head_sem.at[k]),
        )

    def send(src, dst, send_sem, recv_sem, device):
        return pltpu.make_async_remote_copy(
            src_ref=src,
            dst_ref=dst,
            send_sem=send_sem,
            recv_sem=recv_sem,
            device_id={"dp": device},
            device_id_type=MESH,
        )

    def rows_of(row, size):
        return pl.ds(pl.multiple_of(row, h), size)

    def exchange(x):
        return send(give.at[x.p], take.at[x.p], give_sem, take_sem.at[x.p % 3], other)

    def part_copy(x, way):
        src = stage.at[x.p, pl.ds(2 * chunk + way * h, h)]
        return send(src, part.at[x.p, way], stage_sem, part_sem.at[x.p % PARTS], to[way])

    def whole_copy(x, way, piece_half):
        src = stage.at[x.p, pl.ds(way * chunk + piece_half * h, h)]
        dst = whole.at[x.p, way, pl.ds(piece_half * h, h)]
        return send(src, dst, stage_sem, whole_sem.at[x.p % WHOLES], to[way])

    def own_copy(x, way):
        where = x.in_out(chip * chunk, chunk)
        return send(where, where, own_sem, near_sem.at[x.p // 2], to[way])

    def pass_copy(x, way):
        where = x.in_out((prv, nxt)[way] * chunk + way * h, h)
        return send(where, where, pass_sem, far_sem.at[x.p // 2], to[way])

    def last_copy(x, owner):
        where = x.in_out(owner * chunk, chunk)
        return send(where, where, last_sem, done_sem, other)

    def wait_all(ref, sem):
        pltpu.make_async_copy(ref, ref, sem).wait()

    def own_term(x, row, size):
        where = rows_of(row, size)
        return acc[x.acc, where] + take[x.p, where].astype(jnp.float32)

    def begin(x):
        exchange(x).wait_recv()
        stage[x.p, pl.ds(2 * chunk, chunk)] = own_term(x, opp * chunk, chunk).astype(stage.dtype)
        for way in range(2):
            part_copy(x, way).start()
        for way in range(2):
            rest = beside[way] * chunk + (1 - way) * h
            stage[x.p, pl.ds(way * chunk + (1 - way) * h, h)] = own_term(x, rest, h).astype(stage.dtype)
            whole_copy(x, way, 1 - way).start()
        for way in range(2):
            row = beside[way] * chunk + way * h
            acc[x.acc, rows_of(row, h)] = own_term(x, row, h)
        kept[x.p] = own_term(x, chip * chunk, chunk)

    def pass_parts(x):
        wait_all(part.at[x.p], part_sem.at[x.p % PARTS])
        for way in range(2):
            mine = acc[x.acc, rows_of(beside[way] * chunk + way * h, h)]
            total = mine + part[x.p, way].astype(jnp.float32)
            stage[x.p, pl.ds(way * chunk + way * h, h)] = total.astype(stage.dtype)
            whole_copy(x, way, way).start()

    def finish(x):
        wait_all(whole.at[x.p], whole_sem.at[x.p % WHOLES])
        total = kept[x.p]
        for way in range(2):
            total += whole[x.p, way].astype(jnp.float32)
        x.in_out(chip * chunk, chunk)[...] = total.astype(out.dtype)
        for way in range(2):
            own_copy(x, way).start()

    def gather(q):
        wait_all(whole.at[pl.ds(2 * q, 2)], near_sem.at[q])
        for x in (Piece(2 * q), Piece(2 * q + 1)):
            for way in range(2):
                pass_copy(x, way).start()
            for owner in (chip, nxt, prv):
                last_copy(x, owner).start()

    def close(q):
        wait_all(part.at[pl.ds(2 * q, 2)], far_sem.at[q])
        for x in (Piece(2 * q), Piece(2 * q + 1)):
            last_copy(x, opp).start()

    def when(live, do, p):
        pl.when(live & (p >= 0) & (p < pieces))(lambda: do(Piece(p)))

    def product(lhs, rhs):
        return lax.dot_general(lhs, rhs, (((0,), (0,)), ((), ())), preferred_element_type=jnp.float32)

    for k in range(HEAD):
        for copy in head_copies(k):
            copy.start()
    g_copy(1).start()
    barrier = pltpu.get_barrier_semaphore()
    for device in (other, right, left):
        pl.semaphore_signal(barrier, inc=1, device_id={"dp": device}, device_id_type=MESH)
    mine, theirs = rows_of(core * half, half), rows_of((1 - core) * half, half)

    for k in range(HEAD):
        wait_all(gbuf.at[pl.ds(0, 2), pl.ds(0, tokens // HEAD)], head_sem.at[k])
        some = pl.ds(k * (tokens // HEAD), tokens // HEAD)
        terms = product(abuf[0, some, theirs], gbuf[0, some])
        if k < HEAD - 1:
            acc[1] = terms + acc[1] if k else terms
        else:
            give[0] = (terms + acc[1]).astype(give.dtype)
            pl.semaphore_wait(barrier, 3)
            exchange(Piece(0)).start()
        terms = product(abuf[0, some, mine], gbuf[0, some])
        acc[0] = terms + acc[0] if k else terms
    g_copy(2).start()

    def nth(k):
        return k - (k + 1) // 3

    @pl.loop(1, CLOSE + pieces // 2)
    def _(s):
        p, n, c = s, s // blocks, s % blocks

        @pl.when(s < pieces)
        def _():
            @pl.when(p + 2 < pieces)
            def _():
                g_copy(p + 2).start()

            @pl.when((c == 1) & (n + 1 < matrices))
            def _():
                a_copy(n + 1).start()

            @pl.when(c == 0)
            def _():
                a_copy(n).wait()

            g_copy(p).wait()
            give[p] = product(abuf[n % 2, :, theirs], gbuf[p % 3]).astype(give.dtype)
            exchange(Piece(p)).start()

        when(s == 1, begin, 0)
        when(s > 2, pass_parts, s - 2)

        @pl.when(s < pieces)
        def _():
            acc[p % ACCS] = product(abuf[n % 2, :, mine], gbuf[p % 3])

        when(s > 0, begin, s)
        when(s == 2, pass_parts, 0)
        k = s - SPARSE
        when((s < DENSE[0]) & (k >= 0) & (k % 3 != 1), finish, nth(k))
        for i in range(DENSE[1]):
            when(s >= DENSE[0], finish, nth(DENSE[0] - SPARSE) + (s - DENSE[0]) * DENSE[1] + i)
        pl.when((s >= GATHER) & (s < GATHER + pieces // 2))(lambda: gather(s - GATHER))
        pl.when(s >= CLOSE)(lambda: close(s - CLOSE))

    wait_all(give, give_sem)
    wait_all(stage, stage_sem)
    wait_all(whole, own_sem)
    wait_all(part, pass_sem)
    wait_all(take, last_sem)
    wait_all(take, done_sem)


def solution(mesh):
    chips = mesh.shape["dp"] // 2

    def step(a, g):
        _, matrices, tokens, rows = a.shape
        columns = g.shape[-1]
        pieces = matrices * (columns // BLOCK)
        half = rows // 2
        chunk = half // chips
        vmem = lambda *shape: pltpu.VMEM(shape, jnp.bfloat16)
        dma = pltpu.SemaphoreType.DMA
        return pl.pallas_call(
            functools.partial(kernel, chips),
            out_shape=pltpu.VMEM((matrices, rows, columns), jnp.bfloat16),
            in_specs=[pl.BlockSpec(memory_space=pl.ANY)] * 2,
            out_specs=pl.BlockSpec(memory_space=pltpu.VMEM),
            scratch_shapes=[
                vmem(2, tokens, rows),
                vmem(3, tokens, BLOCK),
                pltpu.VMEM((ACCS, half, BLOCK), jnp.float32),
                pltpu.VMEM((pieces, chunk, BLOCK), jnp.float32),
                vmem(pieces, half, BLOCK),
                vmem(pieces, half, BLOCK),
                vmem(pieces, 3 * chunk, BLOCK),
                vmem(pieces, 2, chunk // 2, BLOCK),
                vmem(pieces, 2, chunk, BLOCK),
                dma((HEAD,)),
                dma((2,)),
                dma((3,)),
                dma,
                dma((3,)),
                dma,
                dma((PARTS,)),
                dma((WHOLES,)),
                dma,
                dma((pieces // 2,)),
                dma,
                dma((pieces // 2,)),
                dma,
                dma,
            ],
            compiler_params=pltpu.CompilerParams(
                collective_id=0, has_side_effects=True, vmem_limit_bytes=50 * 2**20
            ),
            name="grad_sums",
        )(a, g)

    return jax.shard_map(
        step,
        mesh=mesh,
        in_specs=(P(("rep", "dp")), P(("rep", "dp"))),
        out_specs=P("rep"),
        check_vma=False,
    )
```

time: 98.8 us -> 86.6 us (0.88)
  Pallas kernels: 90.2 us -> 83.1 us
  local copies, waits for them, and re-layouts: 8.44 us -> 3.4 us
    pallas_call x1, Pallas kernels: 90.2 us -> 83.1 us  [step(): pl.pallas_call(functools.partial(kernel, chips), out_shape=pltpu.VMEM((ma...]
    unnamed x1, local copies, waits for them, and re-layouts: 8.44 us -> 3.4 us
where the time goes in v2:
time: 86.6 us; the launch traced here: 86.5 us
  Pallas kernels  83.1 us (96%)
  local copies, waits for them, and re-layouts  3.4 us (4%)
    pallas_call x1, Pallas kernels, step(): pl.pallas_call(functools.partial(kernel, chips), out_shape=pltpu.VMEM((ma...  83.1 us
    unnamed x1, local copies, waits for them, and re-layouts  3.4 us

profile of v2, /device:TPU:113, one launch (start us, length us, event | category | flops | bytes accessed | tf_op | source)
XLA Modules:
  0.0 86.5 jit_solution(6623324090444466945)
XLA Ops:
  0.0 83.1 %grad_sums.1 = bf16[4,512,2048]{2,1,0:T(8,128)(2,1)S(1)} custom-call(bf16[1,4,4096,512]{3,2,1,0:T(8,128)(2,1)} %a_hbm.1, bf16[1,4,4096,2048]{3,2,1,0:T(8,128)(2,1)} %g_hbm.1), custom_call_target="tpu_custom_call" | custom-call | tf_op jit(solution)/shard_map/grad_sums/pallas_call | solution.py:268
  83.1 3.4 %copy.4 = bf16[4,512,2048]{2,1,0:T(8,128)(2,1)} copy(bf16[4,512,2048]{2,1,0:T(8,128)(2,1)S(1)} %grad_sums.1) | data formatting | bytes 16777216

commit v3 on v2

--- a/solution.py
+++ b/solution.py
@@ -10,12 +10,12 @@
 MESH = pl.DeviceIdType.MESH
 BLOCK = 512
 ACCS = 4
-HEAD = 4
-PARTS, WHOLES = 6, 12
-SPARSE = 4
-DENSE = 15, 3
-GATHER = 17
-CLOSE = 20
+HEAD = 2, 2, 2, 2
+PARTS, WHOLES = 6, 9
+SPARSE = 3
+DENSE = 15, 2
+GATHER = 18
+CLOSE = 21
 
 def kernel(
     chips,
@@ -80,9 +80,12 @@
         cols = pl.ds(pl.multiple_of(p % blocks * BLOCK, BLOCK), BLOCK)
         return pltpu.make_async_copy(g_hbm.at[0, p // blocks, :, cols], gbuf.at[p % 3], g_sem.at[p % 3])
 
+    def head_part(k):
+        unit = tokens // sum(HEAD)
+        return pl.ds(sum(HEAD[:k]) * unit, HEAD[k] * unit)
+
     def head_copies(k):
-        size = tokens // HEAD
-        some = pl.ds(k * size, size)
+        some = head_part(k)
         return (
             pltpu.make_async_copy(a_hbm.at[0, 0, some], abuf.at[0, some], head_sem.at[k]),
             pltpu.make_async_copy(g_hbm.at[0, 0, some, pl.ds(0, BLOCK)], gbuf.at[0, some], head_sem.at[k]),
@@ -182,7 +185,7 @@
     def product(lhs, rhs):
         return lax.dot_general(lhs, rhs, (((0,), (0,)), ((), ())), preferred_element_type=jnp.float32)
 
-    for k in range(HEAD):
+    for k in range(len(HEAD)):
         for copy in head_copies(k):
             copy.start()
     g_copy(1).start()
@@ -191,11 +194,11 @@
         pl.semaphore_signal(barrier, inc=1, device_id={"dp": device}, device_id_type=MESH)
     mine, theirs = rows_of(core * half, half), rows_of((1 - core) * half, half)
 
-    for k in range(HEAD):
-        wait_all(gbuf.at[pl.ds(0, 2), pl.ds(0, tokens // HEAD)], head_sem.at[k])
-        some = pl.ds(k * (tokens // HEAD), tokens // HEAD)
+    for k in range(len(HEAD)):
+        some = head_part(k)
+        wait_all(gbuf.at[pl.ds(0, 2), some], head_sem.at[k])
         terms = product(abuf[0, some, theirs], gbuf[0, some])
-        if k < HEAD - 1:
+        if k < len(HEAD) - 1:
             acc[1] = terms + acc[1] if k else terms
         else:
             give[0] = (terms + acc[1]).astype(give.dtype)
@@ -205,9 +208,6 @@
         acc[0] = terms + acc[0] if k else terms
     g_copy(2).start()
 
-    def nth(k):
-        return k - (k + 1) // 3
-
     @pl.loop(1, CLOSE + pieces // 2)
     def _(s):
         p, n, c = s, s // blocks, s % blocks
@@ -232,17 +232,19 @@
 
         when(s == 1, begin, 0)
         when(s > 2, pass_parts, s - 2)
+        when(s == 4, finish, 0)
 
         @pl.when(s < pieces)
         def _():
             acc[p % ACCS] = product(abuf[n % 2, :, mine], gbuf[p % 3])
 
+        when(s == 2, pass_parts, 0)
         when(s > 0, begin, s)
-        when(s == 2, pass_parts, 0)
         k = s - SPARSE
-        when((s < DENSE[0]) & (k >= 0) & (k % 3 != 1), finish, nth(k))
+        when((s < DENSE[0]) & (k > 0) & (k % 3 != 0), finish, k - k // 3)
+        first = DENSE[0] - SPARSE
         for i in range(DENSE[1]):
-            when(s >= DENSE[0], finish, nth(DENSE[0] - SPARSE) + (s - DENSE[0]) * DENSE[1] + i)
+            when(s >= DENSE[0], finish, first - (first + 2) // 3 + 1 + (s - DENSE[0]) * DENSE[1] + i)
         pl.when((s >= GATHER) & (s < GATHER + pieces // 2))(lambda: gather(s - GATHER))
         pl.when(s >= CLOSE)(lambda: close(s - CLOSE))
 
@@ -280,7 +282,7 @@
                 vmem(pieces, 3 * chunk, BLOCK),
                 vmem(pieces, 2, chunk // 2, BLOCK),
                 vmem(pieces, 2, chunk, BLOCK),
-                dma((HEAD,)),
+                dma((len(HEAD),)),
                 dma((2,)),
                 dma((3,)),
                 dma,

time: 86.6 us -> 85.5 us (0.987)
  Pallas kernels: 83.1 us -> 82.1 us
    pallas_call x1, Pallas kernels: 83.1 us -> 82.1 us  [step(): pl.pallas_call(functools.partial(kernel, chips), out_shape=pltpu.VMEM((ma...]
where the time goes in v3:
time: 85.5 us
  Pallas kernels  82.1 us (96%)
  local copies, waits for them, and re-layouts  3.4 us (4%)
    pallas_call x1, Pallas kernels, step(): pl.pallas_call(functools.partial(kernel, chips), out_shape=pltpu.VMEM((ma...  82.1 us
    unnamed x1, local copies, waits for them, and re-layouts  3.4 us

profile of v3, /device:TPU:113, one launch (start us, length us, event | category | flops | bytes accessed | tf_op | source)
XLA Modules:
  0.0 85.5 jit_solution(3467029378229662915)
XLA Ops:
  0.0 82.1 %grad_sums.1 = bf16[4,512,2048]{2,1,0:T(8,128)(2,1)S(1)} custom-call(bf16[1,4,4096,512]{3,2,1,0:T(8,128)(2,1)} %a_hbm.1, bf16[1,4,4096,2048]{3,2,1,0:T(8,128)(2,1)} %g_hbm.1), custom_call_target="tpu_custom_call" | custom-call | tf_op jit(solution)/shard_map/grad_sums/pallas_call | solution.py:270
  82.1 3.4 %copy.4 = bf16[4,512,2048]{2,1,0:T(8,128)(2,1)} copy(bf16[4,512,2048]{2,1,0:T(8,128)(2,1)S(1)} %grad_sums.1) | data formatting | bytes 16777216

commit v4 on v3

--- a/solution.py
+++ b/solution.py
@@ -91,6 +91,11 @@
             pltpu.make_async_copy(g_hbm.at[0, 0, some, pl.ds(0, BLOCK)], gbuf.at[0, some], head_sem.at[k]),
         )
 
+    def second_copy(k):
+        some = pl.ds(k * (tokens // 2), tokens // 2)
+        g = g_hbm.at[0, 0, some, pl.ds(BLOCK, BLOCK)]
+        return pltpu.make_async_copy(g, gbuf.at[1, some], (g_sem.at[1], a_sem.at[0])[k])
+
     def send(src, dst, send_sem, recv_sem, device):
         return pltpu.make_async_remote_copy(
             src_ref=src,
@@ -144,18 +149,14 @@
             rest = beside[way] * chunk + (1 - way) * h
             stage[x.p, pl.ds(way * chunk + (1 - way) * h, h)] = own_term(x, rest, h).astype(stage.dtype)
             whole_copy(x, way, 1 - way).start()
-        for way in range(2):
-            row = beside[way] * chunk + way * h
-            acc[x.acc, rows_of(row, h)] = own_term(x, row, h)
-        kept[x.p] = own_term(x, chip * chunk, chunk)
 
     def pass_parts(x):
         wait_all(part.at[x.p], part_sem.at[x.p % PARTS])
         for way in range(2):
-            mine = acc[x.acc, rows_of(beside[way] * chunk + way * h, h)]
-            total = mine + part[x.p, way].astype(jnp.float32)
+            total = own_term(x, beside[way] * chunk + way * h, h) + part[x.p, way].astype(jnp.float32)
             stage[x.p, pl.ds(way * chunk + way * h, h)] = total.astype(stage.dtype)
             whole_copy(x, way, way).start()
+        kept[x.p] = own_term(x, chip * chunk, chunk)
 
     def finish(x):
         wait_all(whole.at[x.p], whole_sem.at[x.p % WHOLES])
@@ -188,7 +189,8 @@
     for k in range(len(HEAD)):
         for copy in head_copies(k):
             copy.start()
-    g_copy(1).start()
+    for k in range(2):
+        second_copy(k).start()
     barrier = pltpu.get_barrier_semaphore()
     for device in (other, right, left):
         pl.semaphore_signal(barrier, inc=1, device_id={"dp": device}, device_id_type=MESH)
@@ -208,7 +210,19 @@
         acc[0] = terms + acc[0] if k else terms
     g_copy(2).start()
 
-    @pl.loop(1, CLOSE + pieces // 2)
+    low, high = pl.ds(0, tokens // 2), pl.ds(tokens // 2, tokens // 2)
+    second_copy(0).wait()
+    acc[1] = product(abuf[0, low, theirs], gbuf[1, low])
+    second_copy(1).wait()
+    give[1] = (acc[1] + product(abuf[0, high, theirs], gbuf[1, high])).astype(give.dtype)
+    exchange(Piece(1)).start()
+    begin(Piece(0))
+    g_copy(3).start()
+    a_copy(1).start()
+    acc[1] = product(abuf[0, :, mine], gbuf[1])
+    begin(Piece(1))
+
+    @pl.loop(2, CLOSE + pieces // 2)
     def _(s):
         p, n, c = s, s // blocks, s % blocks
 
@@ -230,7 +244,6 @@
             give[p] = product(abuf[n % 2, :, theirs], gbuf[p % 3]).astype(give.dtype)
             exchange(Piece(p)).start()
 
-        when(s == 1, begin, 0)
         when(s > 2, pass_parts, s - 2)
         when(s == 4, finish, 0)
 

time: 85.5 us -> 85.3 us (level)
  no operation moved by 1% of the time
where the time goes in v4:
time: 85.3 us
  Pallas kernels  81.9 us (96%)
  local copies, waits for them, and re-layouts  3.4 us (4%)
    pallas_call x1, Pallas kernels, step(): pl.pallas_call(functools.partial(kernel, chips), out_shape=pltpu.VMEM((ma...  81.9 us
    unnamed x1, local copies, waits for them, and re-layouts  3.4 us

profile of v4, /device:TPU:113, one launch (start us, length us, event | category | flops | bytes accessed | tf_op | source)
XLA Modules:
  0.0 85.3 jit_solution(6482149133279420034)
XLA Ops:
  0.0 81.9 %grad_sums.1 = bf16[4,512,2048]{2,1,0:T(8,128)(2,1)S(1)} custom-call(bf16[1,4,4096,512]{3,2,1,0:T(8,128)(2,1)} %a_hbm.1, bf16[1,4,4096,2048]{3,2,1,0:T(8,128)(2,1)} %g_hbm.1), custom_call_target="tpu_custom_call" | custom-call | tf_op jit(solution)/shard_map/grad_sums/pallas_call | solution.py:283
  81.9 3.4 %copy.4 = bf16[4,512,2048]{2,1,0:T(8,128)(2,1)} copy(bf16[4,512,2048]{2,1,0:T(8,128)(2,1)S(1)} %grad_sums.1) | data formatting | bytes 16777216

commit v5 on v4

--- a/solution.py
+++ b/solution.py
@@ -15,6 +15,7 @@
 SPARSE = 3
 DENSE = 15, 2
 GATHER = 18
+YIELD = 2
 CLOSE = 21
 
 def kernel(
@@ -258,7 +259,9 @@
         first = DENSE[0] - SPARSE
         for i in range(DENSE[1]):
             when(s >= DENSE[0], finish, first - (first + 2) // 3 + 1 + (s - DENSE[0]) * DENSE[1] + i)
-        pl.when((s >= GATHER) & (s < GATHER + pieces // 2))(lambda: gather(s - GATHER))
+        final = pieces // 2 - 1
+        pl.when((s >= GATHER) & (s < GATHER + final))(lambda: gather(s - GATHER))
+        pl.when(s == GATHER + final + core * YIELD)(lambda: gather(final))
         pl.when(s >= CLOSE)(lambda: close(s - CLOSE))
 
     wait_all(give, give_sem)

time: 85.3 us -> 85.3 us (level)
  no operation moved by 1% of the time
where the time goes in v5:
time: 85.3 us; the launch traced here: 85.2 us
  Pallas kernels  81.8 us (96%)
  local copies, waits for them, and re-layouts  3.4 us (4%)
    pallas_call x1, Pallas kernels, step(): pl.pallas_call(functools.partial(kernel, chips), out_shape=pltpu.VMEM((ma...  81.8 us
    unnamed x1, local copies, waits for them, and re-layouts  3.4 us

profile of v5, /device:TPU:113, one launch (start us, length us, event | category | flops | bytes accessed | tf_op | source)
XLA Modules:
  0.0 85.2 jit_solution(9054698691350771509)
XLA Ops:
  0.0 81.8 %grad_sums.1 = bf16[4,512,2048]{2,1,0:T(8,128)(2,1)S(1)} custom-call(bf16[1,4,4096,512]{3,2,1,0:T(8,128)(2,1)} %a_hbm.1, bf16[1,4,4096,2048]{3,2,1,0:T(8,128)(2,1)} %g_hbm.1), custom_call_target="tpu_custom_call" | custom-call | tf_op jit(solution)/shard_map/grad_sums/pallas_call | solution.py:286
  81.8 3.4 %copy.4 = bf16[4,512,2048]{2,1,0:T(8,128)(2,1)} copy(bf16[4,512,2048]{2,1,0:T(8,128)(2,1)S(1)} %grad_sums.1) | data formatting | bytes 16777216
